TPU v7x, 32 devices: a whole 2x2x4 slice. The times are simulated.
32 devices in a mesh: gx: 8 (over y, x, core), gy: 4 (over z).
Axes of the slice: x: 2, y: 2, z: 4, core: 2. Of those that a mesh axis runs over, the one named last changes fastest.
Arguments:
- east_class: int32 [512, 256], P('gx', 'gy'), may hold values from 0 to 7
- south_class: int32 [512, 256], P('gx', 'gy'), may hold values from 0 to 7
- cond_table: float32 [8], replicated, may hold values from 0.5 to 4
- leakage: float32 [512, 256], P('gx', 'gy'), may hold values from 0.1 to 1
- pad_mask: int32 [512, 256], P('gx', 'gy'), may hold values 0 or 1
- load_current: float32 [512, 256, 256], P('gx', 'gy'), may hold values from -24 to 24
Outputs:
- potential: float32 [512, 256, 256], P('gx', 'gy')
All inputs are finite; a program needn't handle non-finite values. No bound on the sum of `pad_mask` on one device may be relied on, other than what follows from the above.
Results may differ from a plain program's by a relative error of at most 0.00002.
Values sent between devices are 32-bit elements; how exact they have to be, the bound alone decides.
A program may use at most 64 MiB of HBM per device.

v0:
```python
import functools

import jax
import jax.numpy as jnp
from jax import lax
from jax.experimental import pallas as pl
from jax.experimental.pallas import tpu as pltpu
from jax.sharding import PartitionSpec as P

ITERS = 4
PAD_GAIN = 8.0
SPECTRAL_BOUND = 0.995
G = ITERS
MESH = pl.DeviceIdType.MESH


def polynomial():
    weights = [1.0]
    for k in range(1, ITERS):
        if k == 1:
            weights.append(1.0 / (1.0 - SPECTRAL_BOUND**2 / 2.0))
        else:
            weights.append(1.0 / (1.0 - SPECTRAL_BOUND**2 * weights[-1] / 4.0))
    size = ITERS + 1
    previous = [1.0] + [0.0] * (size - 1)
    field = [1.0, 1.0] + [0.0] * (size - 2)
    for k in range(1, ITERS):
        jac = [1.0] + field[:-1]
        updated = [weights[k] * (a - b) + b for a, b in zip(jac, previous)]
        previous, field = field, updated
    return field


def loop(lo, count, width, compute):
    def turn(start, size):
        pending = [compute(start + u) for u in range(size)]
        for stores in pending:
            for put in stores:
                put()

    turns, rest = count // width, count % width
    if turns:
        lax.fori_loop(0, turns, lambda t, c: (turn(lo + t * width, width), c)[1], 0)
    if rest:
        turn(lo + turns * width, rest)


def setter(ref, index, value):
    def put():
        ref[index] = value
    return put


EAST, SOUTH, ROOT, PADS = range(4)


def kernel(
    nx, ny, rows, cols,
    table_hbm, east_hbm, south_hbm, leak_hbm, pad_hbm, x_ref, o_ref,
    table_ref, east_ref, south_ref, leak_ref, pad_ref,
    cf, tw, dn, load, src, v1, v2, v3, bc, eload,
    small_sem, local_sem, send_sem, recv_sem,
):
    mx, my = lax.axis_index("gx"), lax.axis_index("gy")
    north, south = lax.rem(mx + nx - 1, nx), lax.rem(mx + 1, nx)
    west, east = lax.rem(my + ny - 1, ny), lax.rem(my + 1, ny)
    cases = x_ref.shape[2]
    halves = [slice(h * 128, (h + 1) * 128) for h in range(cases // 128)]
    poly = polynomial()

    barrier = pltpu.get_barrier_semaphore()
    peers = [(north, my), (south, my), (mx, west), (mx, east)]
    for peer in peers:
        pl.semaphore_signal(barrier, inc=1, device_id=peer, device_id_type=MESH)
    small = [
        pltpu.make_async_copy(there, here, small_sem.at[n])
        for n, (there, here) in enumerate([
            (table_hbm, table_ref), (east_hbm, east_ref), (south_hbm, south_ref),
            (leak_hbm, leak_ref), (pad_hbm, pad_ref),
        ])
    ]
    for copy in small:
        copy.start()
    own = pltpu.make_async_copy(x_ref, load.at[pl.ds(G, rows)], local_sem)
    own.start()
    for copy in small:
        copy.wait()

    def lookup(classes):
        value = jnp.full(classes.shape, table_ref[0], jnp.float32)
        for c in range(1, table_ref.shape[0]):
            value = jnp.where(classes == c, table_ref[c], value)
        return value

    blank = jnp.zeros((rows, 128 - cols), jnp.float32)
    fields = [
        lookup(east_ref[...]),
        lookup(south_ref[...]),
        leak_ref[...] + PAD_GAIN * pad_ref[...].astype(jnp.float32),
    ]
    for f in range(3):
        cf[f, pl.ds(8, rows), :] = jnp.concatenate([fields[f], blank], axis=1)
    above, below = jnp.zeros((8, 128), jnp.float32), jnp.zeros((120 - rows, 128), jnp.float32)
    for f in range(3):
        square = jnp.concatenate([above, jnp.concatenate([fields[f], blank], axis=1), below], axis=0)
        tw[f, pl.ds(8, cols), :] = jnp.transpose(square)[0:cols, :]

    pl.semaphore_wait(barrier, len(peers))
    own.wait()

    counter = [0]

    def send(source, target, device):
        n = counter[0]
        counter[0] += 1
        copy = pltpu.make_async_remote_copy(
            src_ref=source, dst_ref=target,
            send_sem=send_sem.at[n], recv_sem=recv_sem.at[n],
            device_id=device, device_id_type=MESH,
        )
        copy.start()
        return copy

    def side(count, at):
        return [
            send(
                load.at[pl.ds(at, count), pl.ds(cols - G, G)],
                eload.at[0, pl.ds(at, count), pl.ds(0, G)],
                (mx, east),
            ),
            send(
                load.at[pl.ds(at, count), pl.ds(0, G)],
                eload.at[1, pl.ds(at, count), pl.ds(G, G)],
                (mx, west),
            ),
        ]

    def corner(at, row, width):
        return [
            send(
                load.at[pl.ds(at, row), pl.ds(cols - width, width)],
                eload.at[0, pl.ds(at, row), pl.ds(G - width, width)],
                (mx, east),
            ),
            send(
                load.at[pl.ds(at, row), pl.ds(0, width)],
                eload.at[1, pl.ds(at, row), pl.ds(G, width)],
                (mx, west),
            ),
        ]

    cuts = [G + rows // 2, G + rows // 2 + 3 * rows // 8]
    first = side(cuts[0] - G, G)
    cf_n = send(cf.at[:, pl.ds(rows, 8)], cf.at[:, pl.ds(0, 8)], (south, my))
    cf_s = send(cf.at[:, pl.ds(8, 8)], cf.at[:, pl.ds(rows + 8, 8)], (north, my))
    ld_n = send(load.at[pl.ds(rows, G)], load.at[pl.ds(0, G)], (south, my))
    ld_s = send(load.at[pl.ds(G, G)], load.at[pl.ds(rows + G, G)], (north, my))
    D = G - 1

    def dense(lo, size, edges):
        area = pl.ds(lo, size)
        e, s, extra = (tw[f, area, :] for f in range(3))
        e_west = tw[0, pl.ds(lo - 1, size), :] if edges and lo else pltpu.roll(e, 1, 0)
        total = e + e_west + s + pltpu.roll(s, 1, 1) + extra
        root = lax.rsqrt(total)
        pads = jnp.where(extra > PAD_GAIN / 2, PAD_GAIN, 0.0)
        dn[ROOT, area, :] = root
        dn[PADS, area, :] = pads * root
        dn[SOUTH, area, :] = s * root * pltpu.roll(root, 127, 1)

    def dense_east(lo, size):
        area = pl.ds(lo, size)
        dn[EAST, area, :] = tw[0, area, :] * dn[ROOT, area, :] * dn[ROOT, pl.ds(lo + 1, size), :]

    def spread(start, size, lo, count, width):
        def block(t):
            r = lo + t * width
            amount = 128 - (r + 8 - G)
            for f in range(4):
                value = pltpu.roll(dn[f, pl.ds(start, size), :], amount, 1)
                for u in range(width):
                    bc[f, r + u, pl.ds(start, size)] = jnp.broadcast_to(value[:, u : u + 1], (size, 128))
        lax.fori_loop(0, count // width, lambda t, c: (block(t), c)[1], 0)

    dense(8, cols, False)
    dense_east(8, cols)
    spread(8, cols, G, rows, 8)

    chain = [src, v1, v2, v3]

    def source(lo, count):
        def one(r):
            return [
                setter(src, (r, n, pl.ds(8, cols)), bc[PADS, r, pl.ds(8, cols)] - load[r, :, h] * bc[ROOT, r, pl.ds(8, cols)])
                for n, h in enumerate(halves)
            ]
        loop(lo, count, 2, one)

    def gather(r, at, size):
        coefs = [
            bc[EAST, r, pl.ds(at, size)], bc[EAST, r, pl.ds(at - 1, size)],
            bc[SOUTH, r, pl.ds(at, size)], bc[SOUTH, r - 1, pl.ds(at, size)],
        ]
        return coefs

    def update(k, r, n, at, size, coefs):
        vin = chain[k - 1]
        total = coefs[0] * vin[r, n, pl.ds(at + 1, size)]
        total += coefs[1] * vin[r, n, pl.ds(at - 1, size)]
        total += coefs[2] * vin[r + 1, n, pl.ds(at, size)]
        total += coefs[3] * vin[r - 1, n, pl.ds(at, size)]
        if k == 1:
            total = total * poly[ITERS]
        total = total + poly[ITERS - k] * src[r, n, pl.ds(at, size)]
        if k == ITERS:
            total = total * bc[ROOT, r, pl.ds(at, size)]
        return total

    def step(k, lo, count):
        def one(r):
            stores = []
            coefs = gather(r, 8, cols)
            for n, h in enumerate(halves):
                total = update(k, r, n, 8, cols, coefs)
                if k == ITERS:
                    stores.append(setter(o_ref, (r - G, slice(None), h), total))
                else:
                    stores.append(setter(chain[k], (r, n, pl.ds(8, cols)), total))
            return stores

        loop(lo, count, 2, one)

    cf_n.wait_recv()
    cf_s.wait_recv()
    for f in range(3):
        tw[f, pl.ds(8, cols), :] = jnp.transpose(cf[f])[0:cols, :]
    tw_w = send(tw.at[:, pl.ds(cols + 2, 6)], tw.at[:, pl.ds(2, 6)], (mx, east))
    tw_e = send(tw.at[:, pl.ds(8, G)], tw.at[:, pl.ds(cols + 8, G)], (mx, west))
    second = side(cuts[1] - cuts[0], cuts[0])

    source(G, rows)
    for k in range(1, ITERS):
        step(k, G + k + 1, rows - 2 * k - 1)

    ld_n.wait_recv()
    ld_s.wait_recv()
    first += corner(G - 1, 1, D) + corner(G - D, D - 1, D - 1)
    third = side(rows + G - cuts[1], cuts[1])
    third += corner(rows + G, 1, D) + corner(rows + G + 1, D - 1, D - 1)
    step(ITERS, G + ITERS + 1, rows - 2 * ITERS - 1)

    dense(8, cols, False)
    dense_east(8, cols)
    spread(8, cols, 0, G + 1, G + 1)
    spread(8, cols, rows + G - 1, G + 1, G + 1)
    source(0, G + 1)
    source(rows + G, G)
    for k in range(1, ITERS + 1):
        step(k, k, G + 1)
        step(k, rows + 2 * G - k - G, G)

    tw_w.wait_recv()
    tw_e.wait_recv()
    dense(0, 16, True)
    dense(cols, 16, True)
    dense_east(0, 15)
    dense_east(cols, 15)
    spread(0, 16, 0, rows + 2 * G, 8)
    spread(cols, 16, 0, rows + 2 * G, 8)

    lane_row = lax.broadcasted_iota(jnp.int32, (2 * G, 128), 0)
    starts = [9 - G, 8 + cols - G]
    tiles = [pl.ds(start, 2 * G) for start in starts]
    ghosts = [pl.ds(8 - G, 2 * G), tiles[1]]
    mine = [pl.ds(0, G + 1), pl.ds(cols - G, G)]
    inner = [slice(G - 1, 2 * G), slice(0, G)]

    def edge_source(lo, count):
        def one(r):
            stores = []
            for n, h in enumerate(halves):
                near = pltpu.roll(load[r, pl.ds(0, 2 * G), h], G, 0)
                far = pltpu.roll(load[r, pl.ds(cols - 2 * G, 2 * G), h], G, 0)
                for w in range(2):
                    ghost = lane_row < G if w == 0 else lane_row >= G
                    full = jnp.where(ghost, eload[w, r, :, h], far if w else near)
                    value = bc[PADS, r, ghosts[w]] - full * bc[ROOT, r, ghosts[w]]
                    stores.append(setter(src, (r, n, ghosts[w]), value))
            return stores
        loop(lo, count, 4, one)

    def edge_step(k, lo, count):
        def one(r):
            stores = []
            for w in range(2):
                coefs = gather(r, starts[w], 2 * G)
                for n, h in enumerate(halves):
                    total = update(k, r, n, starts[w], 2 * G, coefs)
                    if k < ITERS:
                        stores.append(setter(chain[k], (r, n, tiles[w]), total))
                    else:
                        stores.append(setter(o_ref, (r - G, mine[w], h), total[inner[w]]))
            return stores

        loop(lo, count, 4, one)

    bounds = [0] + cuts + [rows + 2 * G]
    for m, arrived in enumerate([first, second, third]):
        for copy in arrived:
            copy.wait_recv()
        lo, hi = bounds[m], bounds[m + 1]
        edge_source(lo, hi - lo)
        for k in range(1, ITERS + 1):
            begin = k if m == 0 else lo - k
            edge_step(k, begin, hi - k - begin)
    for copy in [cf_n, cf_s, ld_n, ld_s, tw_w, tw_e] + first + second + third:
        copy.wait_send()


def body(nx, ny, east_class, south_class, cond_table, leakage, pad_mask, load_current):
    rows, cols, cases = load_current.shape
    tall = rows + 2 * G
    f32 = jnp.float32
    halves = cases // 128
    anywhere = pl.BlockSpec(memory_space=pl.ANY)
    copies = 6 + 3 * 2 + 4 * 2
    grid = (tall, halves, cols + 16, 128)
    return pl.pallas_call(
        functools.partial(kernel, nx, ny, rows, cols),
        out_shape=pltpu.VMEM(load_current.shape, f32),
        in_specs=[anywhere] * 6,
        out_specs=pl.BlockSpec(memory_space=pltpu.VMEM),
        scratch_shapes=[
            pltpu.SMEM(cond_table.shape, f32),
            pltpu.VMEM((rows, cols), jnp.int32),
            pltpu.VMEM((rows, cols), jnp.int32),
            pltpu.VMEM((rows, cols), f32),
            pltpu.VMEM((rows, cols), jnp.int32),
            pltpu.VMEM((3, 128, 128), f32),
            pltpu.VMEM((3, cols + 16, 128), f32),
            pltpu.VMEM((4, cols + 16, 128), f32),
            pltpu.VMEM((tall, cols, cases), f32),
            pltpu.VMEM(grid, f32),
            pltpu.VMEM(grid, f32),
            pltpu.VMEM(grid, f32),
            pltpu.VMEM(grid, f32),
            pltpu.VMEM((4, tall, cols + 16, 128), f32),
            pltpu.VMEM((2, tall, 2 * G, cases), f32),
            pltpu.SemaphoreType.DMA((5,)),
            pltpu.SemaphoreType.DMA,
            pltpu.SemaphoreType.DMA((copies,)),
            pltpu.SemaphoreType.DMA((copies,)),
        ],
        compiler_params=pltpu.CompilerParams(
            collective_id=0, has_side_effects=True, vmem_limit_bytes=57 * 2**20,
        ),
    )(cond_table, east_class, south_class, leakage, pad_mask, load_current)


def solution(mesh):
    in_specs = (
        P("gx", "gy"),
        P("gx", "gy"),
        P(),
        P("gx", "gy"),
        P("gx", "gy"),
        P("gx", "gy", None),
    )
    out_specs = P("gx", "gy", None)
    call = functools.partial(body, mesh.shape["gx"], mesh.shape["gy"])
    return jax.shard_map(call, mesh=mesh, in_specs=in_specs, out_specs=out_specs, check_vma=False)
```

profile of v0, /device:TPU:0, one launch (start us, length us, event | category | flops | bytes accessed | tf_op | source)
XLA Modules:
  0.0 29.7 jit_solution(14427002139598581011)
XLA Ops:
  0.0 27.6 %shard_map.64 = f32[64,64,256]{2,1,0:T(8,128)S(1)} custom-call(f32[8]{0:T(128)} %table_hbm.1, s32[64,64]{1,0:T(8,128)} %east_hbm.1, s32[64,64]{1,0:T(8,128)} %south_hbm.1, f32[64,64]{1,0:T(8,128)} %leak_hbm.1, s32[64,64]{1,0:T(8,128)} %pad_hbm.1, f32[64,64,256]{2,1,0:T(8,128)} %x_ref.1), custom_call_target="tpu_custom_call" | custom-call | tf_op jit(solution)/shard_map/pallas_call | solution.py:328
  27.6 2.0 %copy.8 = f32[64,64,256]{2,1,0:T(8,128)} copy(f32[64,64,256]{2,1,0:T(8,128)S(1)} %shard_map.64) | data formatting | bytes 8388608
where the time goes:
time: 29.8 us; the launch traced here: 29.7 us
  Pallas kernels  27.6 us (93%)
  local copies, waits for them, and re-layouts  2.02 us (7%)
    pallas_call x1, Pallas kernels, body(): pl.pallas_call(functools.partial(kernel, nx, ny, rows, cols), out_shape=p...  27.6 us
    unnamed x1, local copies, waits for them, and re-layouts  2.02 us

commit v1 on v0

--- a/solution.py
+++ b/solution.py
@@ -58,7 +58,7 @@
     nx, ny, rows, cols,
     table_hbm, east_hbm, south_hbm, leak_hbm, pad_hbm, x_ref, o_ref,
     table_ref, east_ref, south_ref, leak_ref, pad_ref,
-    cf, tw, dn, load, src, v1, v2, v3, bc, eload,
+    cf, tw, pk, pe, load, src, v1, v2, v3, bc, eload,
     small_sem, local_sem, send_sem, recv_sem,
 ):
     mx, my = lax.axis_index("gx"), lax.axis_index("gy")
@@ -100,10 +100,6 @@
     ]
     for f in range(3):
         cf[f, pl.ds(8, rows), :] = jnp.concatenate([fields[f], blank], axis=1)
-    above, below = jnp.zeros((8, 128), jnp.float32), jnp.zeros((120 - rows, 128), jnp.float32)
-    for f in range(3):
-        square = jnp.concatenate([above, jnp.concatenate([fields[f], blank], axis=1), below], axis=0)
-        tw[f, pl.ds(8, cols), :] = jnp.transpose(square)[0:cols, :]
 
     pl.semaphore_wait(barrier, len(peers))
     own.wait()
@@ -157,34 +153,51 @@
     ld_s = send(load.at[pl.ds(G, G)], load.at[pl.ds(rows + G, G)], (north, my))
     D = G - 1
 
-    def dense(lo, size, edges):
+    lane = lax.broadcasted_iota(jnp.int32, (8, 128), 1)
+
+    def dense(lo, size):
         area = pl.ds(lo, size)
+        e, s, extra = (cf[f, area, :] for f in range(3))
+        root = lax.rsqrt(e + pltpu.roll(e, 1, 1) + s + pltpu.roll(s, 1, 0) + extra)
+        pads = jnp.where(extra > PAD_GAIN / 2, PAD_GAIN, 0.0)
+        left = jnp.broadcast_to(lane[0:1] < cols, (size, 128))
+        values = [e * root * pltpu.roll(root, 127, 1), s * root * pltpu.roll(root, size - 1, 0), root, pads * root]
+        for p in range(2):
+            pk[p, area, :] = jnp.where(left, values[2 * p], pltpu.roll(values[2 * p + 1], cols, 1))
+
+    def dense_edge(lo):
+        area = pl.ds(lo, 16)
         e, s, extra = (tw[f, area, :] for f in range(3))
-        e_west = tw[0, pl.ds(lo - 1, size), :] if edges and lo else pltpu.roll(e, 1, 0)
-        total = e + e_west + s + pltpu.roll(s, 1, 1) + extra
-        root = lax.rsqrt(total)
+        e_west = tw[0, pl.ds(lo - 1, 16), :] if lo else pltpu.roll(e, 1, 0)
+        root = lax.rsqrt(e + e_west + s + pltpu.roll(s, 1, 1) + extra)
         pads = jnp.where(extra > PAD_GAIN / 2, PAD_GAIN, 0.0)
-        dn[ROOT, area, :] = root
-        dn[PADS, area, :] = pads * root
-        dn[SOUTH, area, :] = s * root * pltpu.roll(root, 127, 1)
-
-    def dense_east(lo, size):
-        area = pl.ds(lo, size)
-        dn[EAST, area, :] = tw[0, area, :] * dn[ROOT, area, :] * dn[ROOT, pl.ds(lo + 1, size), :]
-
-    def spread(start, size, lo, count, width):
+        return [e * root * pltpu.roll(root, 15, 0), s * root * pltpu.roll(root, 127, 1), root, pads * root]
+
+    def turned(ref, r):
+        return jnp.transpose(jnp.broadcast_to(ref[pl.ds(r + 8 - G, 1), :], (128, 128)))
+
+    def spread(lo, count, width):
         def block(t):
-            r = lo + t * width
-            amount = 128 - (r + 8 - G)
-            for f in range(4):
-                value = pltpu.roll(dn[f, pl.ds(start, size), :], amount, 1)
-                for u in range(width):
-                    bc[f, r + u, pl.ds(start, size)] = jnp.broadcast_to(value[:, u : u + 1], (size, 128))
+            for u in range(width):
+                r = lo + t * width + u
+                for p in range(2):
+                    value = turned(pk.at[p], r)
+                    bc[2 * p, r, pl.ds(8, cols)] = value[0:cols]
+                    bc[2 * p + 1, r, pl.ds(8, cols)] = value[cols : 2 * cols]
         lax.fori_loop(0, count // width, lambda t, c: (block(t), c)[1], 0)
 
-    dense(8, cols, False)
-    dense_east(8, cols)
-    spread(8, cols, G, rows, 8)
+    def spread_edge(lo, count, width):
+        def block(t):
+            for u in range(width):
+                r = lo + t * width + u
+                value = turned(pe, r)
+                for f in range(4):
+                    bc[f, r, pl.ds(0, 16)] = value[32 * f : 32 * f + 16]
+                    bc[f, r, pl.ds(cols, 16)] = value[32 * f + 16 : 32 * f + 32]
+        lax.fori_loop(0, count // width, lambda t, c: (block(t), c)[1], 0)
+
+    dense(8, rows)
+    spread(G, rows, 8)
 
     chain = [src, v1, v2, v3]
 
@@ -249,10 +262,9 @@
     third += corner(rows + G, 1, D) + corner(rows + G + 1, D - 1, D - 1)
     step(ITERS, G + ITERS + 1, rows - 2 * ITERS - 1)
 
-    dense(8, cols, False)
-    dense_east(8, cols)
-    spread(8, cols, 0, G + 1, G + 1)
-    spread(8, cols, rows + G - 1, G + 1, G + 1)
+    dense(0, rows + 16)
+    spread(0, G + 1, G + 1)
+    spread(rows + G - 1, G + 1, G + 1)
     source(0, G + 1)
     source(rows + G, G)
     for k in range(1, ITERS + 1):
@@ -261,12 +273,9 @@
 
     tw_w.wait_recv()
     tw_e.wait_recv()
-    dense(0, 16, True)
-    dense(cols, 16, True)
-    dense_east(0, 15)
-    dense_east(cols, 15)
-    spread(0, 16, 0, rows + 2 * G, 8)
-    spread(cols, 16, 0, rows + 2 * G, 8)
+    sides = zip(dense_edge(0), dense_edge(cols))
+    pe[...] = jnp.transpose(jnp.concatenate([part for pair in sides for part in pair], axis=0))
+    spread_edge(0, rows + 2 * G, 8)
 
     lane_row = lax.broadcasted_iota(jnp.int32, (2 * G, 128), 0)
     starts = [9 - G, 8 + cols - G]
@@ -338,7 +347,8 @@
             pltpu.VMEM((rows, cols), jnp.int32),
             pltpu.VMEM((3, 128, 128), f32),
             pltpu.VMEM((3, cols + 16, 128), f32),
-            pltpu.VMEM((4, cols + 16, 128), f32),
+            pltpu.VMEM((2, 128, 128), f32),
+            pltpu.VMEM((128, 128), f32),
             pltpu.VMEM((tall, cols, cases), f32),
             pltpu.VMEM(grid, f32),
             pltpu.VMEM(grid, f32),

time: 29.8 us -> 24.4 us (0.82)
  Pallas kernels: 27.6 us -> 22.2 us
    pallas_call x1, Pallas kernels: 27.6 us -> 22.2 us  [body(): pl.pallas_call(functools.partial(kernel, nx, ny, rows, cols), out_shape=p...]
where the time goes in v1:
time: 24.4 us; the launch traced here: 24.2 us
  Pallas kernels  22.2 us (91%)
  local copies, waits for them, and re-layouts  2.02 us (8%)
    pallas_call x1, Pallas kernels, body(): pl.pallas_call(functools.partial(kernel, nx, ny, rows, cols), out_shape=p...  22.2 us
    unnamed x1, local copies, waits for them, and re-layouts  2.02 us

profile of v1, /device:TPU:0, one launch (start us, length us, event | category | flops | bytes accessed | tf_op | source)
XLA Modules:
  0.0 24.2 jit_solution(17899006664912960528)
XLA Ops:
  0.0 22.2 %shard_map.64 = f32[64,64,256]{2,1,0:T(8,128)S(1)} custom-call(f32[8]{0:T(128)} %table_hbm.1, s32[64,64]{1,0:T(8,128)} %east_hbm.1, s32[64,64]{1,0:T(8,128)} %south_hbm.1, f32[64,64]{1,0:T(8,128)} %leak_hbm.1, s32[64,64]{1,0:T(8,128)} %pad_hbm.1, f32[64,64,256]{2,1,0:T(8,128)} %x_ref.1), custom_call_target="tpu_custom_call" | custom-call | tf_op jit(solution)/shard_map/pallas_call | solution.py:337
  22.2 2.0 %copy.8 = f32[64,64,256]{2,1,0:T(8,128)} copy(f32[64,64,256]{2,1,0:T(8,128)S(1)} %shard_map.64) | data formatting | bytes 8388608

commit v2 on v1

--- a/solution.py
+++ b/solution.py
@@ -59,7 +59,7 @@
     table_hbm, east_hbm, south_hbm, leak_hbm, pad_hbm, x_ref, o_ref,
     table_ref, east_ref, south_ref, leak_ref, pad_ref,
     cf, tw, pk, pe, load, src, v1, v2, v3, bc, eload,
-    small_sem, local_sem, send_sem, recv_sem,
+    small_sem, rim_sem, local_sem, send_sem, recv_sem,
 ):
     mx, my = lax.axis_index("gx"), lax.axis_index("gy")
     north, south = lax.rem(mx + nx - 1, nx), lax.rem(mx + 1, nx)
@@ -81,7 +81,14 @@
     ]
     for copy in small:
         copy.start()
-    own = pltpu.make_async_copy(x_ref, load.at[pl.ds(G, rows)], local_sem)
+    area = pl.ds(G, rows)
+    rims = [
+        pltpu.make_async_copy(x_ref.at[:, pl.ds(0, G)], eload.at[0, area, pl.ds(G, G)], rim_sem.at[0]),
+        pltpu.make_async_copy(x_ref.at[:, pl.ds(cols - G, G)], eload.at[1, area, pl.ds(0, G)], rim_sem.at[1]),
+    ]
+    for copy in rims:
+        copy.start()
+    own = pltpu.make_async_copy(x_ref, load.at[area], local_sem)
     own.start()
     for copy in small:
         copy.wait()
@@ -102,7 +109,8 @@
         cf[f, pl.ds(8, rows), :] = jnp.concatenate([fields[f], blank], axis=1)
 
     pl.semaphore_wait(barrier, len(peers))
-    own.wait()
+    for copy in rims:
+        copy.wait()
 
     counter = [0]
 
@@ -117,41 +125,27 @@
         copy.start()
         return copy
 
-    def side(count, at):
+    def side(at, count):
         return [
             send(
-                load.at[pl.ds(at, count), pl.ds(cols - G, G)],
+                eload.at[1, pl.ds(at, count), pl.ds(0, G)],
                 eload.at[0, pl.ds(at, count), pl.ds(0, G)],
                 (mx, east),
             ),
             send(
-                load.at[pl.ds(at, count), pl.ds(0, G)],
+                eload.at[0, pl.ds(at, count), pl.ds(G, G)],
                 eload.at[1, pl.ds(at, count), pl.ds(G, G)],
                 (mx, west),
             ),
         ]
 
-    def corner(at, row, width):
-        return [
-            send(
-                load.at[pl.ds(at, row), pl.ds(cols - width, width)],
-                eload.at[0, pl.ds(at, row), pl.ds(G - width, width)],
-                (mx, east),
-            ),
-            send(
-                load.at[pl.ds(at, row), pl.ds(0, width)],
-                eload.at[1, pl.ds(at, row), pl.ds(G, width)],
-                (mx, west),
-            ),
-        ]
-
-    cuts = [G + rows // 2, G + rows // 2 + 3 * rows // 8]
-    first = side(cuts[0] - G, G)
+    cuts = [G + rows // 2, G + rows // 2 + 5 * rows // 16]
+    ends = side(G, G) + side(rows, G)
+    first = side(2 * G, cuts[0] - 2 * G)
     cf_n = send(cf.at[:, pl.ds(rows, 8)], cf.at[:, pl.ds(0, 8)], (south, my))
     cf_s = send(cf.at[:, pl.ds(8, 8)], cf.at[:, pl.ds(rows + 8, 8)], (north, my))
-    ld_n = send(load.at[pl.ds(rows, G)], load.at[pl.ds(0, G)], (south, my))
-    ld_s = send(load.at[pl.ds(G, G)], load.at[pl.ds(rows + G, G)], (north, my))
-    D = G - 1
+    ld_n = send(x_ref.at[pl.ds(rows - G, G)], load.at[pl.ds(0, G)], (south, my))
+    ld_s = send(x_ref.at[pl.ds(0, G)], load.at[pl.ds(rows + G, G)], (north, my))
 
     lane = lax.broadcasted_iota(jnp.int32, (8, 128), 1)
 
@@ -166,24 +160,31 @@
             pk[p, area, :] = jnp.where(left, values[2 * p], pltpu.roll(values[2 * p + 1], cols, 1))
 
     def dense_edge(lo):
-        area = pl.ds(lo, 16)
+        size = 16 if lo else 24
+        area = pl.ds(lo, size)
         e, s, extra = (tw[f, area, :] for f in range(3))
-        e_west = tw[0, pl.ds(lo - 1, 16), :] if lo else pltpu.roll(e, 1, 0)
+        e_west = tw[0, pl.ds(lo - 1, size), :] if lo else pltpu.roll(e, 1, 0)
         root = lax.rsqrt(e + e_west + s + pltpu.roll(s, 1, 1) + extra)
         pads = jnp.where(extra > PAD_GAIN / 2, PAD_GAIN, 0.0)
-        return [e * root * pltpu.roll(root, 15, 0), s * root * pltpu.roll(root, 127, 1), root, pads * root]
+        values = [e * root * pltpu.roll(root, size - 1, 0), s * root * pltpu.roll(root, 127, 1), root, pads * root]
+        return [value[0:16] for value in values]
 
     def turned(ref, r):
         return jnp.transpose(jnp.broadcast_to(ref[pl.ds(r + 8 - G, 1), :], (128, 128)))
 
     def spread(lo, count, width):
+        inside = pl.ds(8, cols)
+
         def block(t):
             for u in range(width):
                 r = lo + t * width + u
-                for p in range(2):
-                    value = turned(pk.at[p], r)
-                    bc[2 * p, r, pl.ds(8, cols)] = value[0:cols]
-                    bc[2 * p + 1, r, pl.ds(8, cols)] = value[cols : 2 * cols]
+                value = turned(pk.at[0], r)
+                bc[EAST, r, inside] = value[0:cols]
+                bc[SOUTH, r, inside] = value[cols : 2 * cols]
+                value = turned(pk.at[1], r)
+                bc[ROOT, r, inside] = value[0:cols]
+                for n, h in enumerate(halves):
+                    src[r, n, inside] = value[cols : 2 * cols] - load[r, :, h] * value[0:cols]
         lax.fori_loop(0, count // width, lambda t, c: (block(t), c)[1], 0)
 
     def spread_edge(lo, count, width):
@@ -197,17 +198,10 @@
         lax.fori_loop(0, count // width, lambda t, c: (block(t), c)[1], 0)
 
     dense(8, rows)
+    own.wait()
     spread(G, rows, 8)
 
     chain = [src, v1, v2, v3]
-
-    def source(lo, count):
-        def one(r):
-            return [
-                setter(src, (r, n, pl.ds(8, cols)), bc[PADS, r, pl.ds(8, cols)] - load[r, :, h] * bc[ROOT, r, pl.ds(8, cols)])
-                for n, h in enumerate(halves)
-            ]
-        loop(lo, count, 2, one)
 
     def gather(r, at, size):
         coefs = [
@@ -230,15 +224,18 @@
         return total
 
     def step(k, lo, count):
+        skip = 2 * G if k == ITERS else G
+        at, size = 8 + skip, cols - 2 * skip
+
         def one(r):
             stores = []
-            coefs = gather(r, 8, cols)
+            coefs = gather(r, at, size)
             for n, h in enumerate(halves):
-                total = update(k, r, n, 8, cols, coefs)
+                total = update(k, r, n, at, size, coefs)
                 if k == ITERS:
-                    stores.append(setter(o_ref, (r - G, slice(None), h), total))
+                    stores.append(setter(o_ref, (r - G, pl.ds(skip, size), h), total))
                 else:
-                    stores.append(setter(chain[k], (r, n, pl.ds(8, cols)), total))
+                    stores.append(setter(chain[k], (r, n, pl.ds(at, size)), total))
             return stores
 
         loop(lo, count, 2, one)
@@ -249,24 +246,23 @@
         tw[f, pl.ds(8, cols), :] = jnp.transpose(cf[f])[0:cols, :]
     tw_w = send(tw.at[:, pl.ds(cols + 2, 6)], tw.at[:, pl.ds(2, 6)], (mx, east))
     tw_e = send(tw.at[:, pl.ds(8, G)], tw.at[:, pl.ds(cols + 8, G)], (mx, west))
-    second = side(cuts[1] - cuts[0], cuts[0])
-
-    source(G, rows)
-    for k in range(1, ITERS):
+    second = side(cuts[0], cuts[1] - cuts[0])
+    third = side(cuts[1], rows - cuts[1])
+
+    step(1, G + 2, rows - 3)
+    for copy in ends:
+        copy.wait_recv()
+    for w in range(2):
+        first.append(send(eload.at[w, pl.ds(rows, G)], eload.at[w, pl.ds(0, G)], (south, my)))
+        third.append(send(eload.at[w, pl.ds(G, G)], eload.at[w, pl.ds(rows + G, G)], (north, my)))
+    for k in range(2, ITERS + 1):
         step(k, G + k + 1, rows - 2 * k - 1)
 
     ld_n.wait_recv()
     ld_s.wait_recv()
-    first += corner(G - 1, 1, D) + corner(G - D, D - 1, D - 1)
-    third = side(rows + G - cuts[1], cuts[1])
-    third += corner(rows + G, 1, D) + corner(rows + G + 1, D - 1, D - 1)
-    step(ITERS, G + ITERS + 1, rows - 2 * ITERS - 1)
-
     dense(0, rows + 16)
     spread(0, G + 1, G + 1)
     spread(rows + G - 1, G + 1, G + 1)
-    source(0, G + 1)
-    source(rows + G, G)
     for k in range(1, ITERS + 1):
         step(k, k, G + 1)
         step(k, rows + 2 * G - k - G, G)
@@ -277,24 +273,17 @@
     pe[...] = jnp.transpose(jnp.concatenate([part for pair in sides for part in pair], axis=0))
     spread_edge(0, rows + 2 * G, 8)
 
-    lane_row = lax.broadcasted_iota(jnp.int32, (2 * G, 128), 0)
-    starts = [9 - G, 8 + cols - G]
-    tiles = [pl.ds(start, 2 * G) for start in starts]
-    ghosts = [pl.ds(8 - G, 2 * G), tiles[1]]
-    mine = [pl.ds(0, G + 1), pl.ds(cols - G, G)]
-    inner = [slice(G - 1, 2 * G), slice(0, G)]
+    edge = 2 * G
+    rims_at = [[8 - G, 9 - G, 9 - G, 10 - G, 8], [8 + cols - G, 7 + cols - G, 7 + cols - G, 6 + cols - G, 8 + cols - 2 * G]]
 
     def edge_source(lo, count):
         def one(r):
             stores = []
-            for n, h in enumerate(halves):
-                near = pltpu.roll(load[r, pl.ds(0, 2 * G), h], G, 0)
-                far = pltpu.roll(load[r, pl.ds(cols - 2 * G, 2 * G), h], G, 0)
-                for w in range(2):
-                    ghost = lane_row < G if w == 0 else lane_row >= G
-                    full = jnp.where(ghost, eload[w, r, :, h], far if w else near)
-                    value = bc[PADS, r, ghosts[w]] - full * bc[ROOT, r, ghosts[w]]
-                    stores.append(setter(src, (r, n, ghosts[w]), value))
+            for w in range(2):
+                area = pl.ds(rims_at[w][0], edge)
+                pads, root = bc[PADS, r, area], bc[ROOT, r, area]
+                for n, h in enumerate(halves):
+                    stores.append(setter(src, (r, n, area), pads - eload[w, r, :, h] * root))
             return stores
         loop(lo, count, 4, one)
 
@@ -302,13 +291,14 @@
         def one(r):
             stores = []
             for w in range(2):
-                coefs = gather(r, starts[w], 2 * G)
+                at = rims_at[w][k]
+                coefs = gather(r, at, edge)
                 for n, h in enumerate(halves):
-                    total = update(k, r, n, starts[w], 2 * G, coefs)
+                    total = update(k, r, n, at, edge, coefs)
                     if k < ITERS:
-                        stores.append(setter(chain[k], (r, n, tiles[w]), total))
+                        stores.append(setter(chain[k], (r, n, pl.ds(at, edge)), total))
                     else:
-                        stores.append(setter(o_ref, (r - G, mine[w], h), total[inner[w]]))
+                        stores.append(setter(o_ref, (r - G, pl.ds(at - 8, edge), h), total))
             return stores
 
         loop(lo, count, 4, one)
@@ -322,7 +312,7 @@
         for k in range(1, ITERS + 1):
             begin = k if m == 0 else lo - k
             edge_step(k, begin, hi - k - begin)
-    for copy in [cf_n, cf_s, ld_n, ld_s, tw_w, tw_e] + first + second + third:
+    for copy in [cf_n, cf_s, ld_n, ld_s, tw_w, tw_e] + ends + first + second + third:
         copy.wait_send()
 
 
@@ -332,7 +322,7 @@
     f32 = jnp.float32
     halves = cases // 128
     anywhere = pl.BlockSpec(memory_space=pl.ANY)
-    copies = 6 + 3 * 2 + 4 * 2
+    copies = 6 + 5 * 2 + 2 * 2
     grid = (tall, halves, cols + 16, 128)
     return pl.pallas_call(
         functools.partial(kernel, nx, ny, rows, cols),
@@ -357,6 +347,7 @@
             pltpu.VMEM((4, tall, cols + 16, 128), f32),
             pltpu.VMEM((2, tall, 2 * G, cases), f32),
             pltpu.SemaphoreType.DMA((5,)),
+            pltpu.SemaphoreType.DMA((2,)),
             pltpu.SemaphoreType.DMA,
             pltpu.SemaphoreType.DMA((copies,)),
             pltpu.SemaphoreType.DMA((copies,)),

time: 24.4 us -> 22.1 us (0.906)
  Pallas kernels: 22.2 us -> 19.9 us
    pallas_call x1, Pallas kernels: 22.2 us -> 19.9 us  [body(): pl.pallas_call(functools.partial(kernel, nx, ny, rows, cols), out_shape=p...]
where the time goes in v2:
time: 22.1 us; the launch traced here: 21.9 us
  Pallas kernels  19.9 us (90%)
  local copies, waits for them, and re-layouts  2.02 us (9%)
    pallas_call x1, Pallas kernels, body(): pl.pallas_call(functools.partial(kernel, nx, ny, rows, cols), out_shape=p...  19.9 us
    unnamed x1, local copies, waits for them, and re-layouts  2.02 us

profile of v2, /device:TPU:0, one launch (start us, length us, event | category | flops | bytes accessed | tf_op | source)
XLA Modules:
  0.0 21.9 jit_solution(5723715823120563317)
XLA Ops:
  0.0 19.9 %shard_map.64 = f32[64,64,256]{2,1,0:T(8,128)S(1)} custom-call(f32[8]{0:T(128)} %table_hbm.1, s32[64,64]{1,0:T(8,128)} %east_hbm.1, s32[64,64]{1,0:T(8,128)} %south_hbm.1, f32[64,64]{1,0:T(8,128)} %leak_hbm.1, s32[64,64]{1,0:T(8,128)} %pad_hbm.1, f32[64,64,256]{2,1,0:T(8,128)} %x_ref.1), custom_call_target="tpu_custom_call" | custom-call | tf_op jit(solution)/shard_map/pallas_call | solution.py:327
  19.9 2.0 %copy.8 = f32[64,64,256]{2,1,0:T(8,128)} copy(f32[64,64,256]{2,1,0:T(8,128)S(1)} %shard_map.64) | data formatting | bytes 8388608

commit v3 on v2

--- a/solution.py
+++ b/solution.py
@@ -51,7 +51,7 @@
     return put
 
 
-EAST, SOUTH, ROOT, PADS = range(4)
+EAST, SOUTH, ROOT, FLAG = range(4)
 
 
 def kernel(
@@ -125,23 +125,18 @@
         copy.start()
         return copy
 
-    def side(at, count):
-        return [
-            send(
-                eload.at[1, pl.ds(at, count), pl.ds(0, G)],
-                eload.at[0, pl.ds(at, count), pl.ds(0, G)],
-                (mx, east),
-            ),
-            send(
-                eload.at[0, pl.ds(at, count), pl.ds(G, G)],
-                eload.at[1, pl.ds(at, count), pl.ds(G, G)],
-                (mx, west),
-            ),
-        ]
-
-    cuts = [G + rows // 2, G + rows // 2 + 5 * rows // 16]
-    ends = side(G, G) + side(rows, G)
-    first = side(2 * G, cuts[0] - 2 * G)
+    def eastward(at, count):
+        rim = pl.ds(at, count), pl.ds(0, G)
+        return send(eload.at[(1, *rim)], eload.at[(0, *rim)], (mx, east))
+
+    def westward(at, count):
+        rim = pl.ds(at, count), pl.ds(G, G)
+        return send(eload.at[(0, *rim)], eload.at[(1, *rim)], (mx, west))
+
+    cuts = [G + rows // 2, G + 3 * rows // 4, G + rows - 2 * G]
+    mid = G + rows // 4
+    ends = [eastward(G, G), westward(G, G), eastward(rows, G), westward(rows, G)]
+    first = [eastward(2 * G, cuts[0] - 2 * G), westward(2 * G, mid - 2 * G)]
     cf_n = send(cf.at[:, pl.ds(rows, 8)], cf.at[:, pl.ds(0, 8)], (south, my))
     cf_s = send(cf.at[:, pl.ds(8, 8)], cf.at[:, pl.ds(rows + 8, 8)], (north, my))
     ld_n = send(x_ref.at[pl.ds(rows - G, G)], load.at[pl.ds(0, G)], (south, my))
@@ -153,9 +148,10 @@
         area = pl.ds(lo, size)
         e, s, extra = (cf[f, area, :] for f in range(3))
         root = lax.rsqrt(e + pltpu.roll(e, 1, 1) + s + pltpu.roll(s, 1, 0) + extra)
-        pads = jnp.where(extra > PAD_GAIN / 2, PAD_GAIN, 0.0)
+        flagged = jnp.where(extra > PAD_GAIN / 2, -root, root)
         left = jnp.broadcast_to(lane[0:1] < cols, (size, 128))
-        values = [e * root * pltpu.roll(root, 127, 1), s * root * pltpu.roll(root, size - 1, 0), root, pads * root]
+        after = pltpu.roll(root, size - 1, 0)
+        values = [e * root * pltpu.roll(root, 127, 1), s * root * after, flagged, pltpu.roll(flagged, size - 1, 0)]
         for p in range(2):
             pk[p, area, :] = jnp.where(left, values[2 * p], pltpu.roll(values[2 * p + 1], cols, 1))
 
@@ -165,27 +161,31 @@
         e, s, extra = (tw[f, area, :] for f in range(3))
         e_west = tw[0, pl.ds(lo - 1, size), :] if lo else pltpu.roll(e, 1, 0)
         root = lax.rsqrt(e + e_west + s + pltpu.roll(s, 1, 1) + extra)
-        pads = jnp.where(extra > PAD_GAIN / 2, PAD_GAIN, 0.0)
-        values = [e * root * pltpu.roll(root, size - 1, 0), s * root * pltpu.roll(root, 127, 1), root, pads * root]
+        flagged = jnp.where(extra > PAD_GAIN / 2, -root, root)
+        values = [e * root * pltpu.roll(root, size - 1, 0), s * root * pltpu.roll(root, 127, 1), root, flagged]
         return [value[0:16] for value in values]
 
     def turned(ref, r):
         return jnp.transpose(jnp.broadcast_to(ref[pl.ds(r + 8 - G, 1), :], (128, 128)))
 
-    def spread(lo, count, width):
+    def scaled(flagged, value):
+        return jnp.abs(flagged) * (jnp.where(flagged < 0.0, PAD_GAIN, 0.0) - value)
+
+    def spread_rows(lo, count):
         inside = pl.ds(8, cols)
-
-        def block(t):
-            for u in range(width):
-                r = lo + t * width + u
-                value = turned(pk.at[0], r)
-                bc[EAST, r, inside] = value[0:cols]
-                bc[SOUTH, r, inside] = value[cols : 2 * cols]
-                value = turned(pk.at[1], r)
-                bc[ROOT, r, inside] = value[0:cols]
+        stores = []
+        for r in (lo + u for u in range(0, count, 2)):
+            for v in range(2):
+                value = turned(pk.at[0], r + v)
+                stores.append(setter(bc, (EAST, r + v, inside), value[0:cols]))
+                stores.append(setter(bc, (SOUTH, r + v, inside), value[cols : 2 * cols]))
+            both = turned(pk.at[1], r)
+            for v in range(2):
+                value = both[v * cols : (v + 1) * cols]
+                stores.append(setter(bc, (ROOT, r + v, inside), jnp.abs(value)))
                 for n, h in enumerate(halves):
-                    src[r, n, inside] = value[cols : 2 * cols] - load[r, :, h] * value[0:cols]
-        lax.fori_loop(0, count // width, lambda t, c: (block(t), c)[1], 0)
+                    stores.append(setter(src, (r + v, n, inside), scaled(value, load[r + v, :, h])))
+        return stores
 
     def spread_edge(lo, count, width):
         def block(t):
@@ -199,8 +199,6 @@
 
     dense(8, rows)
     own.wait()
-    spread(G, rows, 8)
-
     chain = [src, v1, v2, v3]
 
     def gather(r, at, size):
@@ -223,46 +221,65 @@
             total = total * bc[ROOT, r, pl.ds(at, size)]
         return total
 
-    def step(k, lo, count):
+    def step_row(k, r):
         skip = 2 * G if k == ITERS else G
         at, size = 8 + skip, cols - 2 * skip
-
-        def one(r):
-            stores = []
-            coefs = gather(r, at, size)
-            for n, h in enumerate(halves):
-                total = update(k, r, n, at, size, coefs)
-                if k == ITERS:
-                    stores.append(setter(o_ref, (r - G, pl.ds(skip, size), h), total))
-                else:
-                    stores.append(setter(chain[k], (r, n, pl.ds(at, size)), total))
-            return stores
-
-        loop(lo, count, 2, one)
-
+        stores = []
+        coefs = gather(r, at, size)
+        for n, h in enumerate(halves):
+            total = update(k, r, n, at, size, coefs)
+            if k == ITERS:
+                stores.append(setter(o_ref, (r - G, pl.ds(skip, size), h), total))
+            else:
+                stores.append(setter(chain[k], (r, n, pl.ds(at, size)), total))
+        return stores
+
+    def step(k, lo, count):
+        loop(lo, count, 2, functools.partial(step_row, k))
+
+    W = 8
+    for put in spread_rows(G, W):
+        put()
+
+    def both(t):
+        r = G + W + t * W
+        stores = []
+        for u in range(W):
+            stores += step_row(1, r - W - 1 + u)
+        stores += spread_rows(r, W)
+        for put in stores:
+            put()
+
+    turns = rows // W - 1
+    lax.fori_loop(0, turns, lambda t, c: (both(t), c)[1], 0)
+    step(1, rows + G - W - 1, W)
     cf_n.wait_recv()
     cf_s.wait_recv()
     for f in range(3):
         tw[f, pl.ds(8, cols), :] = jnp.transpose(cf[f])[0:cols, :]
     tw_w = send(tw.at[:, pl.ds(cols + 2, 6)], tw.at[:, pl.ds(2, 6)], (mx, east))
     tw_e = send(tw.at[:, pl.ds(8, G)], tw.at[:, pl.ds(cols + 8, G)], (mx, west))
-    second = side(cuts[0], cuts[1] - cuts[0])
-    third = side(cuts[1], rows - cuts[1])
-
-    step(1, G + 2, rows - 3)
+    second = [eastward(cuts[0], cuts[1] - cuts[0])]
+    third = [eastward(cuts[1], cuts[2] - cuts[1])]
+    fourth = [eastward(cuts[2], rows - cuts[2])]
+    first.append(westward(mid, cuts[0] - mid))
+    second.append(westward(cuts[0], cuts[1] - cuts[0]))
+    third.append(westward(cuts[1], cuts[2] - cuts[1]))
+    fourth.append(westward(cuts[2], rows - cuts[2]))
+
+    for k in range(2, ITERS + 1):
+        step(k, G + k + 1, rows - 2 * k - 1)
+
     for copy in ends:
         copy.wait_recv()
     for w in range(2):
         first.append(send(eload.at[w, pl.ds(rows, G)], eload.at[w, pl.ds(0, G)], (south, my)))
-        third.append(send(eload.at[w, pl.ds(G, G)], eload.at[w, pl.ds(rows + G, G)], (north, my)))
-    for k in range(2, ITERS + 1):
-        step(k, G + k + 1, rows - 2 * k - 1)
-
+        fourth.append(send(eload.at[w, pl.ds(G, G)], eload.at[w, pl.ds(rows + G, G)], (north, my)))
     ld_n.wait_recv()
     ld_s.wait_recv()
     dense(0, rows + 16)
-    spread(0, G + 1, G + 1)
-    spread(rows + G - 1, G + 1, G + 1)
+    for put in spread_rows(0, G + 2) + spread_rows(rows + G - 2, G + 2):
+        put()
     for k in range(1, ITERS + 1):
         step(k, k, G + 1)
         step(k, rows + 2 * G - k - G, G)
@@ -271,7 +288,7 @@
     tw_e.wait_recv()
     sides = zip(dense_edge(0), dense_edge(cols))
     pe[...] = jnp.transpose(jnp.concatenate([part for pair in sides for part in pair], axis=0))
-    spread_edge(0, rows + 2 * G, 8)
+    spread_edge(0, rows + 2 * G, 24)
 
     edge = 2 * G
     rims_at = [[8 - G, 9 - G, 9 - G, 10 - G, 8], [8 + cols - G, 7 + cols - G, 7 + cols - G, 6 + cols - G, 8 + cols - 2 * G]]
@@ -281,9 +298,9 @@
             stores = []
             for w in range(2):
                 area = pl.ds(rims_at[w][0], edge)
-                pads, root = bc[PADS, r, area], bc[ROOT, r, area]
+                flagged = bc[FLAG, r, area]
                 for n, h in enumerate(halves):
-                    stores.append(setter(src, (r, n, area), pads - eload[w, r, :, h] * root))
+                    stores.append(setter(src, (r, n, area), scaled(flagged, eload[w, r, :, h])))
             return stores
         loop(lo, count, 4, one)
 
@@ -304,7 +321,7 @@
         loop(lo, count, 4, one)
 
     bounds = [0] + cuts + [rows + 2 * G]
-    for m, arrived in enumerate([first, second, third]):
+    for m, arrived in enumerate([first, second, third, fourth]):
         for copy in arrived:
             copy.wait_recv()
         lo, hi = bounds[m], bounds[m + 1]
@@ -312,7 +329,7 @@
         for k in range(1, ITERS + 1):
             begin = k if m == 0 else lo - k
             edge_step(k, begin, hi - k - begin)
-    for copy in [cf_n, cf_s, ld_n, ld_s, tw_w, tw_e] + ends + first + second + third:
+    for copy in [cf_n, cf_s, ld_n, ld_s, tw_w, tw_e] + ends + first + second + third + fourth:
         copy.wait_send()
 
 
@@ -322,7 +339,7 @@
     f32 = jnp.float32
     halves = cases // 128
     anywhere = pl.BlockSpec(memory_space=pl.ANY)
-    copies = 6 + 5 * 2 + 2 * 2
+    copies = 6 + 13 + 4
     grid = (tall, halves, cols + 16, 128)
     return pl.pallas_call(
         functools.partial(kernel, nx, ny, rows, cols),

time: 22.1 us -> 21.1 us (0.955)
  Pallas kernels: 19.9 us -> 18.9 us
    pallas_call x1, Pallas kernels: 19.9 us -> 18.9 us  [body(): pl.pallas_call(functools.partial(kernel, nx, ny, rows, cols), out_shape=p...]
where the time goes in v3:
time: 21.1 us; the launch traced here: 20.9 us
  Pallas kernels  18.9 us (90%)
  local copies, waits for them, and re-layouts  2.02 us (10%)
    pallas_call x1, Pallas kernels, body(): pl.pallas_call(functools.partial(kernel, nx, ny, rows, cols), out_shape=p...  18.9 us
    unnamed x1, local copies, waits for them, and re-layouts  2.02 us

profile of v3, /device:TPU:0, one launch (start us, length us, event | category | flops | bytes accessed | tf_op | source)
XLA Modules:
  0.0 20.9 jit_solution(16544478342727235927)
XLA Ops:
  0.0 18.9 %shard_map.64 = f32[64,64,256]{2,1,0:T(8,128)S(1)} custom-call(f32[8]{0:T(128)} %table_hbm.1, s32[64,64]{1,0:T(8,128)} %east_hbm.1, s32[64,64]{1,0:T(8,128)} %south_hbm.1, f32[64,64]{1,0:T(8,128)} %leak_hbm.1, s32[64,64]{1,0:T(8,128)} %pad_hbm.1, f32[64,64,256]{2,1,0:T(8,128)} %x_ref.1), custom_call_target="tpu_custom_call" | custom-call | tf_op jit(solution)/shard_map/pallas_call | solution.py:344
  18.9 2.0 %copy.8 = f32[64,64,256]{2,1,0:T(8,128)} copy(f32[64,64,256]{2,1,0:T(8,128)S(1)} %shard_map.64) | data formatting | bytes 8388608

commit v4 on v3

--- a/solution.py
+++ b/solution.py
@@ -58,7 +58,7 @@
     nx, ny, rows, cols,
     table_hbm, east_hbm, south_hbm, leak_hbm, pad_hbm, x_ref, o_ref,
     table_ref, east_ref, south_ref, leak_ref, pad_ref,
-    cf, tw, pk, pe, load, src, v1, v2, v3, bc, eload,
+    cf, tw, passing, pk, pe, load, src, v1, v2, v3, bc, eload,
     small_sem, rim_sem, local_sem, send_sem, recv_sem,
 ):
     mx, my = lax.axis_index("gx"), lax.axis_index("gy")
@@ -88,7 +88,14 @@
     ]
     for copy in rims:
         copy.start()
-    own = pltpu.make_async_copy(x_ref, load.at[area], local_sem)
+    borders = [
+        pltpu.make_async_copy(x_ref.at[pl.ds(at, G)], load.at[pl.ds(at + G, G)], rim_sem.at[2 + n])
+        for n, at in enumerate([0, rows - G])
+    ]
+    rims += borders
+    for copy in borders:
+        copy.start()
+    own = pltpu.make_async_copy(x_ref.at[pl.ds(G, rows - 2 * G)], load.at[pl.ds(2 * G, rows - 2 * G)], local_sem)
     own.start()
     for copy in small:
         copy.wait()
@@ -108,41 +115,10 @@
     for f in range(3):
         cf[f, pl.ds(8, rows), :] = jnp.concatenate([fields[f], blank], axis=1)
 
-    pl.semaphore_wait(barrier, len(peers))
-    for copy in rims:
-        copy.wait()
-
-    counter = [0]
-
-    def send(source, target, device):
-        n = counter[0]
-        counter[0] += 1
-        copy = pltpu.make_async_remote_copy(
-            src_ref=source, dst_ref=target,
-            send_sem=send_sem.at[n], recv_sem=recv_sem.at[n],
-            device_id=device, device_id_type=MESH,
-        )
-        copy.start()
-        return copy
-
-    def eastward(at, count):
-        rim = pl.ds(at, count), pl.ds(0, G)
-        return send(eload.at[(1, *rim)], eload.at[(0, *rim)], (mx, east))
-
-    def westward(at, count):
-        rim = pl.ds(at, count), pl.ds(G, G)
-        return send(eload.at[(0, *rim)], eload.at[(1, *rim)], (mx, west))
-
-    cuts = [G + rows // 2, G + 3 * rows // 4, G + rows - 2 * G]
-    mid = G + rows // 4
-    ends = [eastward(G, G), westward(G, G), eastward(rows, G), westward(rows, G)]
-    first = [eastward(2 * G, cuts[0] - 2 * G), westward(2 * G, mid - 2 * G)]
-    cf_n = send(cf.at[:, pl.ds(rows, 8)], cf.at[:, pl.ds(0, 8)], (south, my))
-    cf_s = send(cf.at[:, pl.ds(8, 8)], cf.at[:, pl.ds(rows + 8, 8)], (north, my))
-    ld_n = send(x_ref.at[pl.ds(rows - G, G)], load.at[pl.ds(0, G)], (south, my))
-    ld_s = send(x_ref.at[pl.ds(0, G)], load.at[pl.ds(rows + G, G)], (north, my))
-
     lane = lax.broadcasted_iota(jnp.int32, (8, 128), 1)
+
+    def transposed(f):
+        return jnp.transpose(cf[f])[0:cols, :]
 
     def dense(lo, size):
         area = pl.ds(lo, size)
@@ -155,15 +131,22 @@
         for p in range(2):
             pk[p, area, :] = jnp.where(left, values[2 * p], pltpu.roll(values[2 * p + 1], cols, 1))
 
-    def dense_edge(lo):
-        size = 16 if lo else 24
-        area = pl.ds(lo, size)
-        e, s, extra = (tw[f, area, :] for f in range(3))
-        e_west = tw[0, pl.ds(lo - 1, size), :] if lo else pltpu.roll(e, 1, 0)
-        root = lax.rsqrt(e + e_west + s + pltpu.roll(s, 1, 1) + extra)
+    def dense_edge(w, corners):
+        values = []
+        wide = jnp.broadcast_to(lane[0:1], (8, 128))
+        for f in range(3):
+            whole = transposed(f)
+            ghost = tw[f, pl.ds(w * (cols + 8), 8), :]
+            if corners:
+                ghost = jnp.where(wide < 8, pltpu.roll(passing[0, f, pl.ds(8 * w, 8), :], 128 - rows, 1), ghost)
+                ghost = jnp.where(wide < rows + 8, ghost, pltpu.roll(passing[1, f, pl.ds(8 * w, 8), :], rows, 1))
+            parts = [whole[cols - 16 :], ghost] if w else [ghost, whole[0:16]]
+            values.append(jnp.concatenate(parts, axis=0))
+        e, s, extra = values
+        root = lax.rsqrt(e + pltpu.roll(e, 1, 0) + s + pltpu.roll(s, 1, 1) + extra)
         flagged = jnp.where(extra > PAD_GAIN / 2, -root, root)
-        values = [e * root * pltpu.roll(root, size - 1, 0), s * root * pltpu.roll(root, 127, 1), root, flagged]
-        return [value[0:16] for value in values]
+        values = [e * root * pltpu.roll(root, 23, 0), s * root * pltpu.roll(root, 127, 1), root, flagged]
+        return [value[8 * w : 8 * w + 16] for value in values]
 
     def turned(ref, r):
         return jnp.transpose(jnp.broadcast_to(ref[pl.ds(r + 8 - G, 1), :], (128, 128)))
@@ -171,7 +154,7 @@
     def scaled(flagged, value):
         return jnp.abs(flagged) * (jnp.where(flagged < 0.0, PAD_GAIN, 0.0) - value)
 
-    def spread_rows(lo, count):
+    def spread_rows(lo, count, loaded=True):
         inside = pl.ds(8, cols)
         stores = []
         for r in (lo + u for u in range(0, count, 2)):
@@ -183,6 +166,9 @@
             for v in range(2):
                 value = both[v * cols : (v + 1) * cols]
                 stores.append(setter(bc, (ROOT, r + v, inside), jnp.abs(value)))
+                if not loaded:
+                    stores.append(setter(bc, (FLAG, r + v, inside), value))
+                    continue
                 for n, h in enumerate(halves):
                     stores.append(setter(src, (r + v, n, inside), scaled(value, load[r + v, :, h])))
         return stores
@@ -197,8 +183,54 @@
                     bc[f, r, pl.ds(cols, 16)] = value[32 * f + 16 : 32 * f + 32]
         lax.fori_loop(0, count // width, lambda t, c: (block(t), c)[1], 0)
 
+    above, below = jnp.zeros((8, 128), jnp.float32), jnp.zeros((120 - rows, 128), jnp.float32)
+    for f in range(3):
+        square = jnp.concatenate([above, jnp.concatenate([fields[f], blank], axis=1), below], axis=0)
+        tw[f, pl.ds(8, cols), :] = jnp.transpose(square)[0:cols, :]
     dense(8, rows)
-    own.wait()
+    early = 16
+    for put in spread_rows(G, early, False):
+        put()
+
+    pl.semaphore_wait(barrier, len(peers))
+    for copy in rims:
+        copy.wait()
+
+    counter = [0]
+
+    def send(source, target, device):
+        n = counter[0]
+        counter[0] += 1
+        copy = pltpu.make_async_remote_copy(
+            src_ref=source, dst_ref=target,
+            send_sem=send_sem.at[n], recv_sem=recv_sem.at[n],
+            device_id=device, device_id_type=MESH,
+        )
+        copy.start()
+        return copy
+
+    def eastward(at, count):
+        rim = pl.ds(at, count), pl.ds(0, G)
+        return send(eload.at[(1, *rim)], eload.at[(0, *rim)], (mx, east))
+
+    def westward(at, count):
+        rim = pl.ds(at, count), pl.ds(G, G)
+        return send(eload.at[(0, *rim)], eload.at[(1, *rim)], (mx, west))
+
+    cuts = [G + rows // 4, G + rows // 2, G + 3 * rows // 4, G + rows - 2 * G, rows + 2 * G]
+    heads = [2 * G] + cuts[:-1]
+    spans = [(lo, min(hi, rows) - lo) for lo, hi in zip(heads, cuts)]
+    tw_w = send(tw.at[:, pl.ds(cols + 2, 6)], tw.at[:, pl.ds(2, 6)], (mx, east))
+    tw_e = send(tw.at[:, pl.ds(8, G)], tw.at[:, pl.ds(cols + 8, G)], (mx, west))
+    ends = [way(at, G) for way in (eastward, westward) for at in (G, rows)]
+    arrivals = [[eastward(*span)] for span in spans]
+    for part, span in zip(arrivals, spans):
+        part.append(westward(*span))
+    cf_n = send(cf.at[:, pl.ds(rows, 8)], cf.at[:, pl.ds(0, 8)], (south, my))
+    cf_s = send(cf.at[:, pl.ds(8, 8)], cf.at[:, pl.ds(rows + 8, 8)], (north, my))
+    ld_n = send(load.at[pl.ds(rows, G)], load.at[pl.ds(0, G)], (south, my))
+    ld_s = send(load.at[pl.ds(G, G)], load.at[pl.ds(rows + G, G)], (north, my))
+
     chain = [src, v1, v2, v3]
 
     def gather(r, at, size):
@@ -237,12 +269,18 @@
     def step(k, lo, count):
         loop(lo, count, 2, functools.partial(step_row, k))
 
+    own.wait()
+
+    def source_row(r):
+        inside = pl.ds(8, cols)
+        flagged = bc[FLAG, r, inside]
+        return [setter(src, (r, n, inside), scaled(flagged, load[r, :, h])) for n, h in enumerate(halves)]
+
+    loop(G, early, 2, source_row)
     W = 8
-    for put in spread_rows(G, W):
-        put()
 
     def both(t):
-        r = G + W + t * W
+        r = G + early + t * W
         stores = []
         for u in range(W):
             stores += step_row(1, r - W - 1 + u)
@@ -250,45 +288,52 @@
         for put in stores:
             put()
 
-    turns = rows // W - 1
+    if early > W:
+        step(1, G + 2, early - W - 3)
+    turns = (rows - early) // W
     lax.fori_loop(0, turns, lambda t, c: (both(t), c)[1], 0)
     step(1, rows + G - W - 1, W)
+    for k in range(2, ITERS + 1):
+        step(k, G + k + 1, rows - 2 * k - 1)
+        if k == 2:
+            tw_w.wait_recv()
+            tw_e.wait_recv()
+            passed = [
+                send(tw.at[:, pl.ds(at, 8)], passing.at[n, :, pl.ds(8 * w, 8)], (peer, my))
+                for n, peer in enumerate([south, north])
+                for w, at in enumerate([0, cols + 8])
+            ]
+            for copy in ends:
+                copy.wait_recv()
+            for w in range(2):
+                arrivals[0].append(send(eload.at[w, pl.ds(rows, G)], eload.at[w, pl.ds(0, G)], (south, my)))
+                arrivals[-1].append(send(eload.at[w, pl.ds(G, G)], eload.at[w, pl.ds(rows + G, G)], (north, my)))
+
     cf_n.wait_recv()
     cf_s.wait_recv()
-    for f in range(3):
-        tw[f, pl.ds(8, cols), :] = jnp.transpose(cf[f])[0:cols, :]
-    tw_w = send(tw.at[:, pl.ds(cols + 2, 6)], tw.at[:, pl.ds(2, 6)], (mx, east))
-    tw_e = send(tw.at[:, pl.ds(8, G)], tw.at[:, pl.ds(cols + 8, G)], (mx, west))
-    second = [eastward(cuts[0], cuts[1] - cuts[0])]
-    third = [eastward(cuts[1], cuts[2] - cuts[1])]
-    fourth = [eastward(cuts[2], rows - cuts[2])]
-    first.append(westward(mid, cuts[0] - mid))
-    second.append(westward(cuts[0], cuts[1] - cuts[0]))
-    third.append(westward(cuts[1], cuts[2] - cuts[1]))
-    fourth.append(westward(cuts[2], rows - cuts[2]))
-
-    for k in range(2, ITERS + 1):
-        step(k, G + k + 1, rows - 2 * k - 1)
-
-    for copy in ends:
-        copy.wait_recv()
-    for w in range(2):
-        first.append(send(eload.at[w, pl.ds(rows, G)], eload.at[w, pl.ds(0, G)], (south, my)))
-        fourth.append(send(eload.at[w, pl.ds(G, G)], eload.at[w, pl.ds(rows + G, G)], (north, my)))
+    dense(0, rows + 16)
+    for put in spread_rows(0, G + 2, False) + spread_rows(rows + G - 2, G + 2, False):
+        put()
+
+    def edge_fields(corners):
+        sides = zip(dense_edge(0, corners), dense_edge(1, corners))
+        pe[...] = jnp.transpose(jnp.concatenate([part for pair in sides for part in pair], axis=0))
+
+    edge_fields(False)
+    spread_edge(2 * G, rows - 2 * G, 28)
+
     ld_n.wait_recv()
     ld_s.wait_recv()
-    dense(0, rows + 16)
-    for put in spread_rows(0, G + 2) + spread_rows(rows + G - 2, G + 2):
-        put()
+    loop(0, G + 1, 2, source_row)
+    loop(rows + G, G, 2, source_row)
     for k in range(1, ITERS + 1):
         step(k, k, G + 1)
         step(k, rows + 2 * G - k - G, G)
-
-    tw_w.wait_recv()
-    tw_e.wait_recv()
-    sides = zip(dense_edge(0), dense_edge(cols))
-    pe[...] = jnp.transpose(jnp.concatenate([part for pair in sides for part in pair], axis=0))
-    spread_edge(0, rows + 2 * G, 24)
+    for copy in passed:
+        copy.wait_recv()
+    edge_fields(True)
+    spread_edge(0, 2 * G, 2 * G)
+    spread_edge(rows, 2 * G, 2 * G)
 
     edge = 2 * G
     rims_at = [[8 - G, 9 - G, 9 - G, 10 - G, 8], [8 + cols - G, 7 + cols - G, 7 + cols - G, 6 + cols - G, 8 + cols - 2 * G]]
@@ -320,8 +365,8 @@
 
         loop(lo, count, 4, one)
 
-    bounds = [0] + cuts + [rows + 2 * G]
-    for m, arrived in enumerate([first, second, third, fourth]):
+    bounds = [0] + cuts
+    for m, arrived in enumerate(arrivals):
         for copy in arrived:
             copy.wait_recv()
         lo, hi = bounds[m], bounds[m + 1]
@@ -329,7 +374,7 @@
         for k in range(1, ITERS + 1):
             begin = k if m == 0 else lo - k
             edge_step(k, begin, hi - k - begin)
-    for copy in [cf_n, cf_s, ld_n, ld_s, tw_w, tw_e] + ends + first + second + third + fourth:
+    for copy in [cf_n, cf_s, ld_n, ld_s, tw_w, tw_e] + passed + ends + sum(arrivals, []):
         copy.wait_send()
 
 
@@ -339,7 +384,7 @@
     f32 = jnp.float32
     halves = cases // 128
     anywhere = pl.BlockSpec(memory_space=pl.ANY)
-    copies = 6 + 13 + 4
+    copies = 6 + 4 + 10 + 8
     grid = (tall, halves, cols + 16, 128)
     return pl.pallas_call(
         functools.partial(kernel, nx, ny, rows, cols),
@@ -354,6 +399,7 @@
             pltpu.VMEM((rows, cols), jnp.int32),
             pltpu.VMEM((3, 128, 128), f32),
             pltpu.VMEM((3, cols + 16, 128), f32),
+            pltpu.VMEM((2, 3, 16, 128), f32),
             pltpu.VMEM((2, 128, 128), f32),
             pltpu.VMEM((128, 128), f32),
             pltpu.VMEM((tall, cols, cases), f32),
@@ -364,7 +410,7 @@
             pltpu.VMEM((4, tall, cols + 16, 128), f32),
             pltpu.VMEM((2, tall, 2 * G, cases), f32),
             pltpu.SemaphoreType.DMA((5,)),
-            pltpu.SemaphoreType.DMA((2,)),
+            pltpu.SemaphoreType.DMA((4,)),
             pltpu.SemaphoreType.DMA,
             pltpu.SemaphoreType.DMA((copies,)),
             pltpu.SemaphoreType.DMA((copies,)),

time: 21.1 us -> 20.6 us (0.976)
  Pallas kernels: 18.9 us -> 18.4 us
    pallas_call x1, Pallas kernels: 18.9 us -> 18.4 us  [body(): pl.pallas_call(functools.partial(kernel, nx, ny, rows, cols), out_shape=p...]
where the time goes in v4:
time: 20.6 us; the launch traced here: 20.4 us
  Pallas kernels  18.4 us (89%)
  local copies, waits for them, and re-layouts  2.02 us (10%)
    pallas_call x1, Pallas kernels, body(): pl.pallas_call(functools.partial(kernel, nx, ny, rows, cols), out_shape=p...  18.4 us
    unnamed x1, local copies, waits for them, and re-layouts  2.02 us

profile of v4, /device:TPU:0, one launch (start us, length us, event | category | flops | bytes accessed | tf_op | source)
XLA Modules:
  0.0 20.4 jit_solution(10854351791254266872)
XLA Ops:
  0.0 18.4 %shard_map.64 = f32[64,64,256]{2,1,0:T(8,128)S(1)} custom-call(f32[8]{0:T(128)} %table_hbm.1, s32[64,64]{1,0:T(8,128)} %east_hbm.1, s32[64,64]{1,0:T(8,128)} %south_hbm.1, f32[64,64]{1,0:T(8,128)} %leak_hbm.1, s32[64,64]{1,0:T(8,128)} %pad_hbm.1, f32[64,64,256]{2,1,0:T(8,128)} %x_ref.1), custom_call_target="tpu_custom_call" | custom-call | tf_op jit(solution)/shard_map/pallas_call | solution.py:389
  18.4 2.0 %copy.8 = f32[64,64,256]{2,1,0:T(8,128)} copy(f32[64,64,256]{2,1,0:T(8,128)S(1)} %shard_map.64) | data formatting | bytes 8388608

commit v5 on v4

--- a/solution.py
+++ b/solution.py
@@ -58,7 +58,7 @@
     nx, ny, rows, cols,
     table_hbm, east_hbm, south_hbm, leak_hbm, pad_hbm, x_ref, o_ref,
     table_ref, east_ref, south_ref, leak_ref, pad_ref,
-    cf, tw, passing, pk, pe, load, src, v1, v2, v3, bc, eload,
+    cf, tw, passing, rim, pk, pe, load, src, v1, v2, v3, bc, eload,
     small_sem, rim_sem, local_sem, send_sem, recv_sem,
 ):
     mx, my = lax.axis_index("gx"), lax.axis_index("gy")
@@ -67,6 +67,9 @@
     cases = x_ref.shape[2]
     halves = [slice(h * 128, (h + 1) * 128) for h in range(cases // 128)]
     poly = polynomial()
+
+    def settle(view, semaphore):
+        pltpu.make_async_copy(view, view, semaphore).wait()
 
     barrier = pltpu.get_barrier_semaphore()
     peers = [(north, my), (south, my), (mx, west), (mx, east)]
@@ -83,14 +86,14 @@
         copy.start()
     area = pl.ds(G, rows)
     rims = [
-        pltpu.make_async_copy(x_ref.at[:, pl.ds(0, G)], eload.at[0, area, pl.ds(G, G)], rim_sem.at[0]),
-        pltpu.make_async_copy(x_ref.at[:, pl.ds(cols - G, G)], eload.at[1, area, pl.ds(0, G)], rim_sem.at[1]),
+        pltpu.make_async_copy(x_ref.at[:, pl.ds(0, G)], eload.at[0, area, pl.ds(G, G)], rim_sem),
+        pltpu.make_async_copy(x_ref.at[:, pl.ds(cols - G, G)], eload.at[1, area, pl.ds(0, G)], rim_sem),
     ]
     for copy in rims:
         copy.start()
     borders = [
-        pltpu.make_async_copy(x_ref.at[pl.ds(at, G)], load.at[pl.ds(at + G, G)], rim_sem.at[2 + n])
-        for n, at in enumerate([0, rows - G])
+        pltpu.make_async_copy(x_ref.at[pl.ds(at, G)], load.at[pl.ds(at + G, G)], rim_sem)
+        for at in [0, rows - G]
     ]
     rims += borders
     for copy in borders:
@@ -135,18 +138,18 @@
         values = []
         wide = jnp.broadcast_to(lane[0:1], (8, 128))
         for f in range(3):
-            whole = transposed(f)
             ghost = tw[f, pl.ds(w * (cols + 8), 8), :]
             if corners:
                 ghost = jnp.where(wide < 8, pltpu.roll(passing[0, f, pl.ds(8 * w, 8), :], 128 - rows, 1), ghost)
                 ghost = jnp.where(wide < rows + 8, ghost, pltpu.roll(passing[1, f, pl.ds(8 * w, 8), :], rows, 1))
-            parts = [whole[cols - 16 :], ghost] if w else [ghost, whole[0:16]]
-            values.append(jnp.concatenate(parts, axis=0))
+            own_side = rim[f, pl.ds(16 * w, 16), :]
+            values.append(jnp.concatenate([own_side, ghost] if w else [ghost, own_side], axis=0))
         e, s, extra = values
         root = lax.rsqrt(e + pltpu.roll(e, 1, 0) + s + pltpu.roll(s, 1, 1) + extra)
         flagged = jnp.where(extra > PAD_GAIN / 2, -root, root)
-        values = [e * root * pltpu.roll(root, 23, 0), s * root * pltpu.roll(root, 127, 1), root, flagged]
-        return [value[8 * w : 8 * w + 16] for value in values]
+        values = [e * root * pltpu.roll(root, 23, 0), s * root * pltpu.roll(root, 127, 1), flagged]
+        first = 16 - G if w else 8 - G
+        return [value[first : first + 2 * G] for value in values]
 
     def turned(ref, r):
         return jnp.transpose(jnp.broadcast_to(ref[pl.ds(r + 8 - G, 1), :], (128, 128)))
@@ -165,7 +168,7 @@
             both = turned(pk.at[1], r)
             for v in range(2):
                 value = both[v * cols : (v + 1) * cols]
-                stores.append(setter(bc, (ROOT, r + v, inside), jnp.abs(value)))
+                stores.append(setter(bc, (ROOT, r + v, inside), jnp.abs(value) * poly[ITERS]))
                 if not loaded:
                     stores.append(setter(bc, (FLAG, r + v, inside), value))
                     continue
@@ -175,12 +178,17 @@
 
     def spread_edge(lo, count, width):
         def block(t):
-            for u in range(width):
+            for u in range(0, width, 2):
                 r = lo + t * width + u
                 value = turned(pe, r)
-                for f in range(4):
-                    bc[f, r, pl.ds(0, 16)] = value[32 * f : 32 * f + 16]
-                    bc[f, r, pl.ds(cols, 16)] = value[32 * f + 16 : 32 * f + 32]
+                for v in range(2):
+                    for w, at in enumerate([8 - G, 8 + cols - G]):
+                        area = pl.ds(at, 2 * G)
+                        e, s, flagged = (value[64 * v + 8 * (3 * w + f) :][: 2 * G] for f in range(3))
+                        bc[EAST, r + v, area] = e
+                        bc[SOUTH, r + v, area] = s
+                        bc[FLAG, r + v, area] = flagged
+                        bc[ROOT, r + v, area] = jnp.abs(flagged) * poly[ITERS]
         lax.fori_loop(0, count // width, lambda t, c: (block(t), c)[1], 0)
 
     above, below = jnp.zeros((8, 128), jnp.float32), jnp.zeros((120 - rows, 128), jnp.float32)
@@ -193,43 +201,39 @@
         put()
 
     pl.semaphore_wait(barrier, len(peers))
-    for copy in rims:
-        copy.wait()
-
-    counter = [0]
-
-    def send(source, target, device):
-        n = counter[0]
-        counter[0] += 1
+    settle(load.at[pl.ds(0, 4 * G)], rim_sem)
+
+    def send(source, target, device, group, bulk=1):
         copy = pltpu.make_async_remote_copy(
             src_ref=source, dst_ref=target,
-            send_sem=send_sem.at[n], recv_sem=recv_sem.at[n],
+            send_sem=send_sem.at[bulk], recv_sem=recv_sem.at[group],
             device_id=device, device_id_type=MESH,
         )
         copy.start()
-        return copy
-
-    def eastward(at, count):
-        rim = pl.ds(at, count), pl.ds(0, G)
-        return send(eload.at[(1, *rim)], eload.at[(0, *rim)], (mx, east))
-
-    def westward(at, count):
-        rim = pl.ds(at, count), pl.ds(G, G)
-        return send(eload.at[(0, *rim)], eload.at[(1, *rim)], (mx, west))
-
-    cuts = [G + rows // 4, G + rows // 2, G + 3 * rows // 4, G + rows - 2 * G, rows + 2 * G]
+
+    def eastward(at, count, group):
+        part = pl.ds(at, count), pl.ds(0, G)
+        send(eload.at[(1, *part)], eload.at[(0, *part)], (mx, east), group)
+
+    def westward(at, count, group):
+        part = pl.ds(at, count), pl.ds(G, G)
+        send(eload.at[(0, *part)], eload.at[(1, *part)], (mx, west), group)
+
+    cuts = [G + rows * part // 8 for part in (2, 4, 5, 6, 7)] + [rows]
     heads = [2 * G] + cuts[:-1]
-    spans = [(lo, min(hi, rows) - lo) for lo, hi in zip(heads, cuts)]
-    tw_w = send(tw.at[:, pl.ds(cols + 2, 6)], tw.at[:, pl.ds(2, 6)], (mx, east))
-    tw_e = send(tw.at[:, pl.ds(8, G)], tw.at[:, pl.ds(cols + 8, G)], (mx, west))
-    ends = [way(at, G) for way in (eastward, westward) for at in (G, rows)]
-    arrivals = [[eastward(*span)] for span in spans]
-    for part, span in zip(arrivals, spans):
-        part.append(westward(*span))
-    cf_n = send(cf.at[:, pl.ds(rows, 8)], cf.at[:, pl.ds(0, 8)], (south, my))
-    cf_s = send(cf.at[:, pl.ds(8, 8)], cf.at[:, pl.ds(rows + 8, 8)], (north, my))
-    ld_n = send(load.at[pl.ds(rows, G)], load.at[pl.ds(0, G)], (south, my))
-    ld_s = send(load.at[pl.ds(G, G)], load.at[pl.ds(rows + G, G)], (north, my))
+    spans = [(lo, hi - lo) for lo, hi in zip(heads, cuts)]
+    send(tw.at[:, pl.ds(cols + 2, 6)], tw.at[:, pl.ds(2, 6)], (mx, east), 0, 0)
+    send(tw.at[:, pl.ds(8, G)], tw.at[:, pl.ds(cols + 8, G)], (mx, west), 0, 0)
+    for way in (eastward, westward):
+        way(G, G, 1)
+        way(rows, G, 1)
+    for way in (eastward, westward):
+        for n, span in enumerate(spans):
+            way(*span, 5 + n)
+    send(cf.at[:, pl.ds(rows, 8)], cf.at[:, pl.ds(0, 8)], (south, my), 2, 0)
+    send(cf.at[:, pl.ds(8, 8)], cf.at[:, pl.ds(rows + 8, 8)], (north, my), 2, 0)
+    send(load.at[pl.ds(rows, G)], load.at[pl.ds(0, G)], (south, my), 3)
+    send(load.at[pl.ds(G, G)], load.at[pl.ds(rows + G, G)], (north, my), 3)
 
     chain = [src, v1, v2, v3]
 
@@ -246,9 +250,7 @@
         total += coefs[1] * vin[r, n, pl.ds(at - 1, size)]
         total += coefs[2] * vin[r + 1, n, pl.ds(at, size)]
         total += coefs[3] * vin[r - 1, n, pl.ds(at, size)]
-        if k == 1:
-            total = total * poly[ITERS]
-        total = total + poly[ITERS - k] * src[r, n, pl.ds(at, size)]
+        total = total + poly[ITERS - k] / poly[ITERS] * src[r, n, pl.ds(at, size)]
         if k == ITERS:
             total = total * bc[ROOT, r, pl.ds(at, size)]
         return total
@@ -296,41 +298,37 @@
     for k in range(2, ITERS + 1):
         step(k, G + k + 1, rows - 2 * k - 1)
         if k == 2:
-            tw_w.wait_recv()
-            tw_e.wait_recv()
-            passed = [
-                send(tw.at[:, pl.ds(at, 8)], passing.at[n, :, pl.ds(8 * w, 8)], (peer, my))
-                for n, peer in enumerate([south, north])
-                for w, at in enumerate([0, cols + 8])
-            ]
-            for copy in ends:
-                copy.wait_recv()
+            settle(cf.at[:, pl.ds(0, 6 + G)], recv_sem.at[0])
+            for n, peer in enumerate([south, north]):
+                for w, at in enumerate([0, cols + 8]):
+                    send(tw.at[:, pl.ds(at, 8)], passing.at[n, :, pl.ds(8 * w, 8)], (peer, my), 4, 0)
+            settle(eload.at[0, pl.ds(0, 2 * G)], recv_sem.at[1])
             for w in range(2):
-                arrivals[0].append(send(eload.at[w, pl.ds(rows, G)], eload.at[w, pl.ds(0, G)], (south, my)))
-                arrivals[-1].append(send(eload.at[w, pl.ds(G, G)], eload.at[w, pl.ds(rows + G, G)], (north, my)))
-
-    cf_n.wait_recv()
-    cf_s.wait_recv()
+                send(eload.at[w, pl.ds(rows, G)], eload.at[w, pl.ds(0, G)], (south, my), 5)
+                send(eload.at[w, pl.ds(G, G)], eload.at[w, pl.ds(rows + G, G)], (north, my), 5)
+
+    settle(cf.at[:, pl.ds(0, 16)], recv_sem.at[2])
     dense(0, rows + 16)
     for put in spread_rows(0, G + 2, False) + spread_rows(rows + G - 2, G + 2, False):
         put()
 
     def edge_fields(corners):
-        sides = zip(dense_edge(0, corners), dense_edge(1, corners))
-        pe[...] = jnp.transpose(jnp.concatenate([part for pair in sides for part in pair], axis=0))
-
+        stack = jnp.concatenate(dense_edge(0, corners) + dense_edge(1, corners) + [jnp.zeros((16, 128), jnp.float32)], axis=0)
+        pe[...] = jnp.transpose(jnp.concatenate([stack, pltpu.roll(stack, 127, 1)], axis=0))
+
+    for f in range(3):
+        whole = transposed(f)
+        rim[f] = jnp.concatenate([whole[0:16], whole[cols - 16 :]], axis=0)
     edge_fields(False)
     spread_edge(2 * G, rows - 2 * G, 28)
 
-    ld_n.wait_recv()
-    ld_s.wait_recv()
+    settle(load.at[pl.ds(0, 2 * G)], recv_sem.at[3])
     loop(0, G + 1, 2, source_row)
     loop(rows + G, G, 2, source_row)
     for k in range(1, ITERS + 1):
         step(k, k, G + 1)
         step(k, rows + 2 * G - k - G, G)
-    for copy in passed:
-        copy.wait_recv()
+    settle(cf.at[:, pl.ds(0, 32)], recv_sem.at[4])
     edge_fields(True)
     spread_edge(0, 2 * G, 2 * G)
     spread_edge(rows, 2 * G, 2 * G)
@@ -366,16 +364,21 @@
         loop(lo, count, 4, one)
 
     bounds = [0] + cuts
-    for m, arrived in enumerate(arrivals):
-        for copy in arrived:
-            copy.wait_recv()
+    for m, (_, count) in enumerate(spans):
+        settle(eload.at[0, pl.ds(0, count if m else count + 4 * G)], recv_sem.at[5 + m])
         lo, hi = bounds[m], bounds[m + 1]
+        last = m == len(spans) - 1
         edge_source(lo, hi - lo)
         for k in range(1, ITERS + 1):
             begin = k if m == 0 else lo - k
-            edge_step(k, begin, hi - k - begin)
-    for copy in [cf_n, cf_s, ld_n, ld_s, tw_w, tw_e] + passed + ends + sum(arrivals, []):
-        copy.wait_send()
+            edge_step(k, begin, (hi + k if last else hi - k) - begin)
+        if m == 0:
+            edge_source(rows, 2 * G)
+            for k in range(1, G):
+                edge_step(k, rows + k, 2 * G - 2 * k)
+    settle(cf.at[:, pl.ds(0, 6 + G + 16 + 32)], send_sem.at[0])
+    sent = 2 * rows * G + 2 * G * cols + 4 * G * 2 * G
+    settle(load.at[pl.ds(0, sent // cols)], send_sem.at[1])
 
 
 def body(nx, ny, east_class, south_class, cond_table, leakage, pad_mask, load_current):
@@ -384,7 +387,6 @@
     f32 = jnp.float32
     halves = cases // 128
     anywhere = pl.BlockSpec(memory_space=pl.ANY)
-    copies = 6 + 4 + 10 + 8
     grid = (tall, halves, cols + 16, 128)
     return pl.pallas_call(
         functools.partial(kernel, nx, ny, rows, cols),
@@ -400,6 +402,7 @@
             pltpu.VMEM((3, 128, 128), f32),
             pltpu.VMEM((3, cols + 16, 128), f32),
             pltpu.VMEM((2, 3, 16, 128), f32),
+            pltpu.VMEM((3, 32, 128), f32),
             pltpu.VMEM((2, 128, 128), f32),
             pltpu.VMEM((128, 128), f32),
             pltpu.VMEM((tall, cols, cases), f32),
@@ -410,10 +413,10 @@
             pltpu.VMEM((4, tall, cols + 16, 128), f32),
             pltpu.VMEM((2, tall, 2 * G, cases), f32),
             pltpu.SemaphoreType.DMA((5,)),
-            pltpu.SemaphoreType.DMA((4,)),
             pltpu.SemaphoreType.DMA,
-            pltpu.SemaphoreType.DMA((copies,)),
-            pltpu.SemaphoreType.DMA((copies,)),
+            pltpu.SemaphoreType.DMA,
+            pltpu.SemaphoreType.DMA((2,)),
+            pltpu.SemaphoreType.DMA((11,)),
         ],
         compiler_params=pltpu.CompilerParams(
             collective_id=0, has_side_effects=True, vmem_limit_bytes=57 * 2**20,

time: 20.6 us -> 19.8 us (0.961)
  Pallas kernels: 18.4 us -> 17.6 us
    pallas_call x1, Pallas kernels: 18.4 us -> 17.6 us  [body(): pl.pallas_call(functools.partial(kernel, nx, ny, rows, cols), out_shape=p...]
where the time goes in v5:
time: 19.8 us; the launch traced here: 19.6 us
  Pallas kernels  17.6 us (89%)
  local copies, waits for them, and re-layouts  2.02 us (10%)
    pallas_call x1, Pallas kernels, body(): pl.pallas_call(functools.partial(kernel, nx, ny, rows, cols), out_shape=p...  17.6 us
    unnamed x1, local copies, waits for them, and re-layouts  2.02 us

profile of v5, /device:TPU:0, one launch (start us, length us, event | category | flops | bytes accessed | tf_op | source)
XLA Modules:
  0.0 19.6 jit_solution(1865170114054095038)
XLA Ops:
  0.0 17.6 %shard_map.64 = f32[64,64,256]{2,1,0:T(8,128)S(1)} custom-call(f32[8]{0:T(128)} %table_hbm.1, s32[64,64]{1,0:T(8,128)} %east_hbm.1, s32[64,64]{1,0:T(8,128)} %south_hbm.1, f32[64,64]{1,0:T(8,128)} %leak_hbm.1, s32[64,64]{1,0:T(8,128)} %pad_hbm.1, f32[64,64,256]{2,1,0:T(8,128)} %x_ref.1), custom_call_target="tpu_custom_call" | custom-call | tf_op jit(solution)/shard_map/pallas_call | solution.py:391
  17.6 2.0 %copy.8 = f32[64,64,256]{2,1,0:T(8,128)} copy(f32[64,64,256]{2,1,0:T(8,128)S(1)} %shard_map.64) | data formatting | bytes 8388608

commit v6 on v5

--- a/solution.py
+++ b/solution.py
@@ -297,7 +297,7 @@
     step(1, rows + G - W - 1, W)
     for k in range(2, ITERS + 1):
         step(k, G + k + 1, rows - 2 * k - 1)
-        if k == 2:
+        if k == 3:
             settle(cf.at[:, pl.ds(0, 6 + G)], recv_sem.at[0])
             for n, peer in enumerate([south, north]):
                 for w, at in enumerate([0, cols + 8]):

time: 19.8 us -> 19.8 us (level)
  no operation moved by 1% of the time
where the time goes in v6:
time: 19.8 us; the launch traced here: 19.6 us
  Pallas kernels  17.6 us (89%)
  local copies, waits for them, and re-layouts  2.02 us (10%)
    pallas_call x1, Pallas kernels, body(): pl.pallas_call(functools.partial(kernel, nx, ny, rows, cols), out_shape=p...  17.6 us
    unnamed x1, local copies, waits for them, and re-layouts  2.02 us

profile of v6, /device:TPU:0, one launch (start us, length us, event | category | flops | bytes accessed | tf_op | source)
XLA Modules:
  0.0 19.6 jit_solution(1960310066308270675)
XLA Ops:
  0.0 17.6 %shard_map.64 = f32[64,64,256]{2,1,0:T(8,128)S(1)} custom-call(f32[8]{0:T(128)} %table_hbm.1, s32[64,64]{1,0:T(8,128)} %east_hbm.1, s32[64,64]{1,0:T(8,128)} %south_hbm.1, f32[64,64]{1,0:T(8,128)} %leak_hbm.1, s32[64,64]{1,0:T(8,128)} %pad_hbm.1, f32[64,64,256]{2,1,0:T(8,128)} %x_ref.1), custom_call_target="tpu_custom_call" | custom-call | tf_op jit(solution)/shard_map/pallas_call | solution.py:391
  17.6 2.0 %copy.8 = f32[64,64,256]{2,1,0:T(8,128)} copy(f32[64,64,256]{2,1,0:T(8,128)S(1)} %shard_map.64) | data formatting | bytes 8388608
